TPU v7x, 32 devices: a whole 2x2x4 slice. The times are simulated.
32 devices in a mesh: dp: 8 (over y, x, core), mp: 4 (over z).
Axes of the slice: x: 2, y: 2, z: 4, core: 2. Of those that a mesh axis runs over, the one named last changes fastest.
Arguments:
- candidates: bfloat16 [64, 256, 768], P('dp', 'mp'), may hold values from -6 to 6
- owner_row: int32 [64], replicated, may hold values from 0 to 63, as said below
- selected: int32 [16], replicated, may hold values from 0 to 63, as said below
- dest_slot: int32 [16], replicated, may hold values from 0 to 15, as said below
- patch_weight: bfloat16 [768, 768], P(None, 'mp'), may hold values from -0.21875 to 0.21875
- positions: bfloat16 [256, 768], P(None, 'mp'), may hold values from -3 to 3
- qkv_weight: bfloat16 [768, 3, 768], P(None, None, 'mp'), may hold values from -1 to 1
- out_weight: bfloat16 [768, 768], P('mp'), may hold values from -0.21875 to 0.21875
- attn_gain: bfloat16 [768], replicated, may hold values from 0.099609375 to 1.8984375
- mlp_gain: bfloat16 [768], replicated, may hold values from 0.099609375 to 1.8984375
- up_weight: bfloat16 [768, 3072], P(None, 'mp'), may hold values from -0.21875 to 0.21875
- down_weight: bfloat16 [3072, 768], P('mp'), may hold values from -0.109375 to 0.109375
Outputs:
- layer_out: bfloat16 [16, 256, 768], P('dp', 'mp')
Inputs may be any that keep to these rules, and one draw needn't show every extreme that they name: `owner_row`: a permutation; storage row r sits on index r // 8 of dp. `selected`: distinct candidates; no index of dp stores more than 4 of them, and some index stores exactly 4. `dest_slot`: a permutation; the 2 slots s with equal s // 2 get candidates stored on different indices of dp.
All inputs are finite; a program needn't handle non-finite values.
Results may differ from a plain program's by a relative error of at most 0.012.
Values may be sent and summed in bfloat16 or wider, within the bound.
No kernel may reach another device: no remote copies, remote signals or barrier semaphores. Data moves between devices by JAX's collectives and lax.ppermute only.
A program may use at most 128 MiB of HBM per device.

v0:
```python
import jax
import jax.numpy as jnp
from jax import lax
from jax.sharding import PartitionSpec as P

PATCHES = 256
CAND_DEV = 8
SEL_DEV = 2
HEAD_DIM = 64


def norm_rows(values, gain):
    average = jnp.mean(values, axis=-1, keepdims=True)
    centred = values - average
    variance = jnp.mean(centred * centred, axis=-1, keepdims=True)
    return centred * lax.rsqrt(variance + 1e-06) * gain.astype(jnp.float32)


def local(
    candidates,
    owner_row,
    selected,
    dest_slot,
    patch_weight,
    positions,
    qkv_weight,
    out_weight,
    attn_gain,
    mlp_gain,
    up_weight,
    down_weight,
):
    learners = lax.axis_size("dp")
    own_index = lax.axis_index("dp")
    quarter = candidates.shape[1]
    pixel_width = candidates.shape[2]
    chosen_rows = jnp.take(owner_row, selected)
    slot_rows = jnp.zeros(dest_slot.shape, jnp.int32).at[dest_slot].set(chosen_rows)
    source_owner = slot_rows // CAND_DEV
    local_row = slot_rows % CAND_DEV
    stored = candidates.reshape(CAND_DEV, quarter * pixel_width)
    mine = (source_owner == own_index).reshape(learners, SEL_DEV)
    picked = jnp.sum(jnp.where(mine, local_row.reshape(learners, SEL_DEV), 0), axis=1)
    outgoing = jnp.take(stored, picked, axis=0)
    incoming = lax.all_to_all(outgoing, "dp", split_axis=0, concat_axis=0, tiled=True)
    senders = lax.dynamic_slice_in_dim(source_owner, own_index * SEL_DEV, SEL_DEV)
    arrived = jnp.take(incoming, senders, axis=0)
    own_pixels = arrived.reshape(SEL_DEV, quarter, pixel_width)
    product = jnp.einsum(
        "brp,pe->bre",
        lax.all_gather(own_pixels, "mp", axis=1, tiled=True),
        patch_weight,
        preferred_element_type=jnp.float32,
    )
    embedded = (product + positions.astype(jnp.float32)[None]).astype(jnp.bfloat16)
    activations = lax.all_gather(embedded, "mp", axis=2, tiled=True).astype(jnp.float32)
    normed = norm_rows(activations, attn_gain).astype(jnp.bfloat16)
    projected = jnp.einsum(
        "btd,dce->btce", normed, qkv_weight, preferred_element_type=jnp.float32
    ).astype(jnp.bfloat16)
    local_heads = qkv_weight.shape[2] // HEAD_DIM
    head_split = projected.reshape(SEL_DEV, PATCHES, 3, local_heads, HEAD_DIM)
    queries = head_split[:, :, 0]
    attn_keys = head_split[:, :, 1]
    attn_values = head_split[:, :, 2]
    scores = jnp.einsum(
        "bqhd,bkhd->bhqk", queries, attn_keys, preferred_element_type=jnp.float32
    ) * HEAD_DIM ** (-0.5)
    attn_probs = jax.nn.softmax(scores, axis=-1).astype(jnp.bfloat16)
    context = jnp.einsum(
        "bhqk,bkhd->bqhd", attn_probs, attn_values, preferred_element_type=jnp.float32
    ).astype(jnp.bfloat16)
    context = context.reshape(SEL_DEV, PATCHES, local_heads * HEAD_DIM)
    partial_out = jnp.einsum("bte,ed->btd", context, out_weight, preferred_element_type=jnp.float32)
    attended = lax.psum(partial_out.astype(jnp.bfloat16), "mp").astype(jnp.float32)
    after_attn = activations + attended
    normed2 = norm_rows(after_attn, mlp_gain).astype(jnp.bfloat16)
    hidden = jax.nn.gelu(
        jnp.einsum("btd,df->btf", normed2, up_weight, preferred_element_type=jnp.float32),
        approximate=False,
    ).astype(jnp.bfloat16)
    down_terms = jnp.einsum("btf,fd->btd", hidden, down_weight, preferred_element_type=jnp.float32)
    summed = lax.psum_scatter(
        down_terms.astype(jnp.bfloat16), "mp", scatter_dimension=1, tiled=True
    ).astype(jnp.float32)
    residual = lax.dynamic_slice_in_dim(after_attn, lax.axis_index("mp") * quarter, quarter, 1)
    return (residual + summed).astype(jnp.bfloat16)


def solution(mesh):
    return jax.shard_map(
        local,
        mesh=mesh,
        in_specs=(
            P("dp", "mp", None),
            P(),
            P(),
            P(),
            P(None, "mp"),
            P(None, "mp"),
            P(None, None, "mp"),
            P("mp", None),
            P(),
            P(),
            P(None, "mp"),
            P("mp", None),
        ),
        out_specs=P("dp", "mp", None),
        check_vma=False,
    )
```

profile of v0, /device:TPU:0, one launch (start us, length us, event | category | flops | bytes accessed | tf_op | source)
XLA Modules:
  0.0 183.8 jit_solution(13271876456663978697)
XLA Ops:
  6.5 0.0 copy-start
  6.5 0.8 compare_select_fusion.3
  7.3 1.3 gather_fusion
  8.6 0.7 compare_select_fusion.4
  9.3 0.6 scatter_custom_fusion
  9.9 0.1 select_n.81
  10.0 0.1 reduce_sum.56
  10.2 1.6 copy.77
  11.8 1.1 gather_fusion.1
  12.8 0.1 bitcast_select_fusion
  13.0 0.5 broadcast.218
  13.5 1.2 reduce.4
  14.7 0.0 copy-start.5
  14.7 0.0 copy-start.6
  14.7 1.5 reshape.149
  16.2 5.2 %all-to-all-start = ((bf16[8,2,24576]{2,1,0:T(2,128)(2,1)}), bf16[8,2,24576]{2,1,0:T(2,128)(2,1)S(1)}, u32[]{:S(2)}, u32[]{:S(2)}) async-start(bf16[8,2,24576]{2,1,0:T(2,128)(2,1)} %reshape.149), calls=%async_computation | async-start | bytes 1572864 | tf_op jit(solution)/shard_map/all_to_all | solution.py:45
  21.4 0.0 all-reduce.4.cloned.1.call-start
  21.5 0.0 copy-done.5
  21.5 0.7 convert_element_type.51
  22.2 0.0 copy-done.6
  22.2 0.1 compare_and_fusion.1
  22.3 11.7 %all-to-all-done = bf16[8,2,24576]{2,1,0:T(2,128)(2,1)S(1)} async-done(((bf16[8,2,24576]{2,1,0:T(2,128)(2,1)}), bf16[8,2,24576]{2,1,0:T(2,128)(2,1)S(1)}, u32[]{:S(2)}, u32[]{:S(2)}) %all-to-all-start) | async-done | bytes 786464 | tf_op jit(solution)/shard_map/all_to_all | solution.py:45
  34.0 0.8 reshape.150
  34.8 0.9 copy.82
  35.7 0.0 copy-start.2
  35.7 0.0 copy-start.4
  35.7 0.8 gather_fusion.2
  36.5 0.1 bitcast_select_fusion.1
  36.6 18.1 %all_gather.6 = bf16[2,256,768]{2,1,0:T(8,128)(2,1)S(1)} all-gather(bf16[2,64,768]{2,1,0:T(8,128)(2,1)S(1)} %bitcast_select_fusion.1), channel_id=1, replica_groups=mesh['dp'=8,'mp'=4] {'mp'}, dimensions={1}, use_global_device_ids=true | all-gather | bytes 983040 | tf_op jit(solution)/shard_map/all_gather | solution.py:51
  54.7 0.0 copy-done.2
  54.7 0.0 copy-done.4
  54.7 0.4 fusion.20
  55.1 0.2 copy.63
  55.3 17.4 %all_gather.7 = bf16[2,256,768]{1,0,2:T(2,128)(2,1)S(1)} all-gather(bf16[2,256,192]{1,0,2:T(2,128)(2,1)S(1)} %copy.63), channel_id=1, replica_groups=mesh['dp'=8,'mp'=4] {'mp'}, dimensions={2}, use_global_device_ids=true | all-gather | bytes 983040 | tf_op jit(solution)/shard_map/all_gather | solution.py:56
  72.7 0.6 copy.64
  73.3 0.0 copy-start.9
  73.3 0.2 convert_reduce_fusion
  73.5 0.4 fusion.4
  73.9 0.6 copy-done.9
  74.5 0.8 convolution_convert_fusion.2
  75.3 0.7 fusion.108
  76.0 0.9 convolution_convert_fusion.3
  76.9 0.1 copy-done.3
  76.9 1.3 convolution_convert_fusion.1
  78.3 0.0 all-reduce.4.cloned.1.call-update
  78.3 0.2 all-reduce.6.cloned.1.call-start
  78.5 0.0 copy-done.7
  78.5 44.0 %all-reduce.4.cloned.1.call-done = bf16[2,256,768]{2,1,0:T(8,128)(2,1)} async-done(((bf16[2,256,768]{2,1,0:T(8,128)(2,1)}), bf16[2,256,768]{2,1,0:T(8,128)(2,1)}) %all-reduce.4.cloned.1.call-update) | async-done | bytes 786448 | tf_op jit(solution)/shard_map/psum | solution.py:75
  122.5 1.5 fusion.107
  124.0 0.0 copy-done.1
  124.0 0.4 multiply_reduce_fusion
  124.4 0.0 copy-done
  124.4 0.0 copy-start.8
  124.5 1.3 fusion.63
  125.7 0.0 copy-done.8
  125.7 4.4 %convolution_convert_fusion = bf16[2,256,768]{2,1,0:T(8,128)(2,1)S(1)} fusion(bf16[768,768]{1,0:T(8,128)(2,1)S(1)} %copy-done.8, f32[2,256,768]{2,1,0:T(8,128)S(1)} %get-tuple-element.13, u8[256,768]{1,0:T(8,128)(4,1)S(1)} %get-tuple-element.6, u8[256,768]{1,0:T(8,128)(4,1)S(1)} %get-tuple-element.5), kind=kOutput, calls=%fused_computation.41 | convolution fusion | flops 631898112 | bytes 3932160 | tf_op jit(solution)/shard_map/btf,fd->btd/dot_general | solution.py:82
  130.2 0.0 copy-start.10
  130.2 1.7 copy.69
  131.9 0.0 all-reduce.6.cloned.1.call-update
  131.9 0.0 copy-done.10
  131.9 0.6 dynamic-slice
  133.2 42.0 %all-reduce.6.cloned.1.call-done = bf16[2,256,768]{2,0,1:T(2,128)(2,1)} async-done(((bf16[2,256,768]{2,0,1:T(2,128)(2,1)}), bf16[2,256,768]{2,0,1:T(2,128)(2,1)}) %all-reduce.6.cloned.1.call-update) | async-done | bytes 786448
  175.2 1.1 constant_dynamic-slice_fusion
  176.3 0.7 add_convert_fusion
  (15 shorter events, 0.1 us)
Async XLA Ops:
  6.5 117.9 %copy-start = (bf16[768,768]{1,0:T(8,128)(2,1)S(1)}, bf16[768,768]{1,0:T(8,128)(2,1)}, u32[]{:S(2)}) copy-start(bf16[768,768]{1,0:T(8,128)(2,1)} %param.22) | copy-start | bytes 3538948
  14.7 6.8 %copy-start.5 = (bf16[256,192]{0,1:T(8,128)(2,1)S(1)}, bf16[256,192]{0,1:T(8,128)(2,1)}, u32[]{:S(2)}) copy-start(bf16[256,192]{0,1:T(8,128)(2,1)} %param.17) | copy-start | bytes 294916
  14.7 7.5 %copy-start.6 = (bf16[768]{0:T(1024)(128)(2,1)S(1)}, bf16[768]{0:T(1024)(128)(2,1)}, u32[]{:S(2)}) copy-start(bf16[768]{0:T(1024)(128)(2,1)} %param.20) | copy-start | bytes 4612
  16.2 17.8 %all-to-all-start = ((bf16[8,2,24576]{2,1,0:T(2,128)(2,1)}), bf16[8,2,24576]{2,1,0:T(2,128)(2,1)S(1)}, u32[]{:S(2)}, u32[]{:S(2)}) async-start(bf16[8,2,24576]{2,1,0:T(2,128)(2,1)} %reshape.149), calls=%async_computation | async-start | bytes 1572864 | tf_op jit(solution)/shard_map/all_to_all | solution.py:45
  21.4 101.1 %all-reduce.4.cloned.1.call-start = ((), (), s32[]{:S(2)}) async-start(), calls=%async_computation.1 | async-start | bytes 1572864 | tf_op jit(solution)/shard_map/psum | solution.py:75
  35.7 19.0 %copy-start.2 = (f32[256,192]{0,1:T(8,128)S(1)}, f32[256,192]{0,1:T(8,128)}, u32[]{:S(2)}) copy-start(f32[256,192]{0,1:T(8,128)} %convert_element_type.51) | copy-start | bytes 589828
  35.7 19.0 %copy-start.4 = (bf16[768,192]{0,1:T(8,128)(2,1)S(1)}, bf16[768,192]{0,1:T(8,128)(2,1)}, u32[]{:S(2)}) copy-start(bf16[768,192]{0,1:T(8,128)(2,1)} %param.16) | copy-start | bytes 884740
  73.3 1.2 copy-start.9
  76.0 1.0 copy-start.3
  76.9 1.6 copy-start.7
  78.3 96.9 %all-reduce.6.cloned.1.call-start = ((), (), s32[]{:S(2)}) async-start(), calls=%async_computation.2 | async-start | bytes 1572864
  122.5 1.5 copy-start.1
  124.4 1.3 copy-start.8
  130.2 1.8 copy-start.10
Sparse Core Ops, SparseCore 0:
  78.4 44.0 all-reduce.3
  132.0 43.1 all-reduce.5
where the time goes:
time: 184 us
  waiting for transfers between devices  97.8 us (53%)
  blocking collectives  35.5 us (19%)
  between operations  14.3 us (8%)
  local copies, waits for them, and re-layouts  14 us (8%)
  matrix products  9.79 us (5%)
  other arithmetic  7.02 us (4%)
  starting transfers between devices  5.46 us (3%)
    psum x1, waiting for transfers between devices, local(): lax.psum(partial_out.astype(jnp.bfloat16), 'mp').astype(jnp.float32)  44 us
    unnamed x3, waiting for transfers between devices  42.1 us
    all_gather x1, blocking collectives, local(): lax.all_gather(own_pixels, 'mp', axis=1, tiled=True)  18.1 us
    all_gather x1, blocking collectives, local(): lax.all_gather(embedded, 'mp', axis=2, tiled=True).astype(jnp.float32)  17.4 us
    all_to_all x1, waiting for transfers between devices, local(): lax.all_to_all(outgoing, 'dp', split_axis=0, concat_axis=0, tiled=True)  11.7 us
    unnamed x28, local copies, waits for them, and re-layouts  7.11 us
    all_to_all x1, starting transfers between devices, local(): lax.all_to_all(outgoing, 'dp', split_axis=0, concat_axis=0, tiled=True)  5.2 us
    dot_general x1, matrix products, local(): jnp.einsum('btf,fd->btd', hidden, down_weight, preferred_element_type=jnp...  4.43 us
  transfers between devices with their start and end apart: 3, of which 3 were waited for; matrix products, arithmetic and copies ran while one was open for 1% of the time, Pallas kernels for 0%

commit v1 on v0

--- a/solution.py
+++ b/solution.py
@@ -48,7 +48,9 @@
     own_pixels = arrived.reshape(SEL_DEV, quarter, pixel_width)
     product = jnp.einsum(
         "brp,pe->bre",
-        lax.all_gather(own_pixels, "mp", axis=1, tiled=True),
+        jnp.concatenate(
+            lax.all_to_all(jnp.stack([own_pixels] * lax.axis_size("mp")), "mp", 0, 0), axis=1
+        ),
         patch_weight,
         preferred_element_type=jnp.float32,
     )

time: 184 us -> 190 us (1.033)
  waiting for transfers between devices: 97.8 us -> 116 us
  blocking collectives: 35.5 us -> 17.7 us
  starting transfers between devices: 5.46 us -> 10.4 us
    all_gather x1 -> x0, blocking collectives: 18.1 us -> none  [local(): lax.all_gather(own_pixels, 'mp', axis=1, tiled=True)]
    all_to_all x0 -> x1, waiting for transfers between devices: none -> 17.3 us  [local(): lax.all_to_all(jnp.stack([own_pixels] * lax.axis_size('mp')), 'mp', 0, 0)]
    all_to_all x0 -> x1, starting transfers between devices: none -> 5 us  [local(): lax.all_to_all(jnp.stack([own_pixels] * lax.axis_size('mp')), 'mp', 0, 0)]
    unnamed x28 -> x26, local copies, waits for them, and re-layouts: 7.11 us -> 7.1 us
  transfers between devices with their start and end apart: 3 -> 4, of which waited for: 3 -> 4; matrix products, arithmetic and copies ran while one was open for 1% -> 0% of each run, Pallas kernels for 0% -> 0%
where the time goes in v1:
time: 190 us
  waiting for transfers between devices  116 us (61%)
  blocking collectives  17.7 us (9%)
  local copies, waits for them, and re-layouts  15 us (8%)
  between operations  14.3 us (8%)
  starting transfers between devices  10.4 us (5%)
  matrix products  9.78 us (5%)
  other arithmetic  6.35 us (3%)
    psum x1, waiting for transfers between devices, local(): lax.psum(partial_out.astype(jnp.bfloat16), 'mp').astype(jnp.float32)  44.4 us
    unnamed x3, waiting for transfers between devices  42.1 us
    all_gather x1, blocking collectives, local(): lax.all_gather(embedded, 'mp', axis=2, tiled=True).astype(jnp.float32)  17.7 us
    all_to_all x1, waiting for transfers between devices, local(): lax.all_to_all(jnp.stack([own_pixels] * lax.axis_size('mp')), 'mp', 0, 0)  17.3 us
    all_to_all x1, waiting for transfers between devices, local(): lax.all_to_all(outgoing, 'dp', split_axis=0, concat_axis=0, tiled=True)  12.5 us
    unnamed x26, local copies, waits for them, and re-layouts  7.1 us
    all_to_all x1, starting transfers between devices, local(): lax.all_to_all(outgoing, 'dp', split_axis=0, concat_axis=0, tiled=True)  5.2 us
    all_to_all x1, starting transfers between devices, local(): lax.all_to_all(jnp.stack([own_pixels] * lax.axis_size('mp')), 'mp', 0, 0)  5 us
  transfers between devices with their start and end apart: 4, of which 4 were waited for; matrix products, arithmetic and copies ran while one was open for 0% of the time, Pallas kernels for 0%

profile of v1, /device:TPU:0, one launch (start us, length us, event | category | flops | bytes accessed | tf_op | source)
XLA Modules:
  0.0 189.8 jit_solution(10244595845617814187)
XLA Ops:
  6.5 0.0 copy-start
  6.5 0.8 compare_select_fusion.3
  7.3 1.3 gather_fusion
  8.6 0.7 compare_select_fusion.4
  9.3 0.6 scatter_custom_fusion
  9.9 0.1 select_n.82
  10.0 0.1 reduce_sum.56
  10.2 1.6 copy.81
  11.8 1.1 gather_fusion.1
  12.8 0.1 bitcast_select_fusion
  13.0 0.5 broadcast.222
  13.5 1.2 reduce.4
  14.7 1.5 reshape.161
  16.2 5.2 %all-to-all-start = ((bf16[8,2,24576]{2,1,0:T(2,128)(2,1)}), bf16[8,2,24576]{2,1,0:T(2,128)(2,1)S(1)}, u32[]{:S(2)}, u32[]{:S(2)}) async-start(bf16[8,2,24576]{2,1,0:T(2,128)(2,1)} %reshape.161), calls=%async_computation | async-start | bytes 1572864 | tf_op jit(solution)/shard_map/all_to_all | solution.py:45
  21.4 0.1 compare_and_fusion.1
  21.5 12.5 %all-to-all-done = bf16[8,2,24576]{2,1,0:T(2,128)(2,1)S(1)} async-done(((bf16[8,2,24576]{2,1,0:T(2,128)(2,1)}), bf16[8,2,24576]{2,1,0:T(2,128)(2,1)S(1)}, u32[]{:S(2)}, u32[]{:S(2)}) %all-to-all-start) | async-done | bytes 786464 | tf_op jit(solution)/shard_map/all_to_all | solution.py:45
  34.0 0.8 reshape.162
  34.8 0.9 copy.86
  35.7 0.8 gather_fusion.2
  36.5 0.0 copy-start.4
  36.5 0.0 copy-start.5
  36.5 0.1 bitcast_select_fusion.1
  36.6 0.9 stack.3
  37.5 5.0 %all-to-all-start.1 = ((bf16[4,2,64,768]{3,2,1,0:T(8,128)(2,1)}), bf16[4,2,64,768]{3,2,1,0:T(8,128)(2,1)S(1)}, u32[]{:S(2)}, u32[]{:S(2)}) async-start(bf16[4,2,64,768]{3,2,1,0:T(8,128)(2,1)} %stack.3), calls=%async_computation.1 | async-start | bytes 1572864 | tf_op jit(solution)/shard_map/all_to_all | solution.py:52
  42.5 0.0 all-reduce.4.cloned.1.call-start
  42.5 0.0 copy-done.4
  42.6 0.0 copy-done.5
  42.6 17.3 %all-to-all-done.1 = bf16[4,2,64,768]{3,2,1,0:T(8,128)(2,1)S(1)} async-done(((bf16[4,2,64,768]{3,2,1,0:T(8,128)(2,1)}), bf16[4,2,64,768]{3,2,1,0:T(8,128)(2,1)S(1)}, u32[]{:S(2)}, u32[]{:S(2)}) %all-to-all-start.1) | async-done | bytes 786464 | tf_op jit(solution)/shard_map/all_to_all | solution.py:52
  59.9 0.1 copy.66
  60.0 0.0 copy-done.3
  60.0 0.4 fusion.20
  60.4 0.2 copy.67
  60.6 17.7 %all_gather.3 = bf16[2,256,768]{1,0,2:T(2,128)(2,1)S(1)} all-gather(bf16[2,256,192]{1,0,2:T(2,128)(2,1)S(1)} %copy.67), channel_id=1, replica_groups=mesh['dp'=8,'mp'=4] {'mp'}, dimensions={2}, use_global_device_ids=true | all-gather | bytes 983040 | tf_op jit(solution)/shard_map/all_gather | solution.py:58
  78.3 0.6 copy.68
  78.9 0.0 copy-start.8
  78.9 0.2 convert_reduce_fusion
  79.1 0.4 fusion.4
  79.5 0.6 copy-done.8
  80.0 0.8 convolution_convert_fusion.2
  80.9 0.7 fusion.108
  81.5 0.9 convolution_convert_fusion.3
  82.4 0.0 copy-start.6
  82.4 0.1 copy-done.2
  82.5 1.3 convolution_convert_fusion.1
  83.8 0.0 all-reduce.4.cloned.1.call-update
  83.8 0.2 all-reduce.6.cloned.1.call-start
  84.1 0.0 copy-done.6
  84.1 44.4 %all-reduce.4.cloned.1.call-done = bf16[2,256,768]{2,1,0:T(8,128)(2,1)} async-done(((bf16[2,256,768]{2,1,0:T(8,128)(2,1)}), bf16[2,256,768]{2,1,0:T(8,128)(2,1)}) %all-reduce.4.cloned.1.call-update) | async-done | bytes 786448 | tf_op jit(solution)/shard_map/psum | solution.py:77
  128.5 1.5 fusion.107
  129.9 0.0 copy-done.1
  130.0 0.4 multiply_reduce_fusion
  130.4 0.0 copy-done
  130.4 0.0 copy-start.7
  130.4 1.3 fusion.63
  131.7 0.0 copy-done.7
  131.7 4.4 %convolution_convert_fusion = bf16[2,256,768]{2,1,0:T(8,128)(2,1)S(1)} fusion(bf16[768,768]{1,0:T(8,128)(2,1)S(1)} %copy-done.7, f32[2,256,768]{2,1,0:T(8,128)S(1)} %get-tuple-element.13, u8[256,768]{1,0:T(8,128)(4,1)S(1)} %get-tuple-element.6, u8[256,768]{1,0:T(8,128)(4,1)S(1)} %get-tuple-element.5), kind=kOutput, calls=%fused_computation.41 | convolution fusion | flops 631898112 | bytes 3932160 | tf_op jit(solution)/shard_map/btf,fd->btd/dot_general | solution.py:84
  136.1 0.0 copy-start.9
  136.1 1.7 copy.73
  137.9 0.0 all-reduce.6.cloned.1.call-update
  137.9 0.0 copy-done.9
  137.9 0.6 dynamic-slice
  139.1 42.0 %all-reduce.6.cloned.1.call-done = bf16[2,256,768]{2,0,1:T(2,128)(2,1)} async-done(((bf16[2,256,768]{2,0,1:T(2,128)(2,1)}), bf16[2,256,768]{2,0,1:T(2,128)(2,1)}) %all-reduce.6.cloned.1.call-update) | async-done | bytes 786448
  181.2 1.1 constant_dynamic-slice_fusion
  182.2 0.7 add_convert_fusion
  (16 shorter events, 0.1 us)
Async XLA Ops:
  6.5 123.8 %copy-start = (bf16[768,768]{1,0:T(8,128)(2,1)S(1)}, bf16[768,768]{1,0:T(8,128)(2,1)}, u32[]{:S(2)}) copy-start(bf16[768,768]{1,0:T(8,128)(2,1)} %param.22) | copy-start | bytes 3538948
  16.2 17.8 %all-to-all-start = ((bf16[8,2,24576]{2,1,0:T(2,128)(2,1)}), bf16[8,2,24576]{2,1,0:T(2,128)(2,1)S(1)}, u32[]{:S(2)}, u32[]{:S(2)}) async-start(bf16[8,2,24576]{2,1,0:T(2,128)(2,1)} %reshape.161), calls=%async_computation | async-start | bytes 1572864 | tf_op jit(solution)/shard_map/all_to_all | solution.py:45
  36.5 6.1 %copy-start.4 = (bf16[256,192]{0,1:T(8,128)(2,1)S(1)}, bf16[256,192]{0,1:T(8,128)(2,1)}, u32[]{:S(2)}) copy-start(bf16[256,192]{0,1:T(8,128)(2,1)} %param.17) | copy-start | bytes 294916
  36.5 6.1 %copy-start.5 = (bf16[768]{0:T(1024)(128)(2,1)S(1)}, bf16[768]{0:T(1024)(128)(2,1)}, u32[]{:S(2)}) copy-start(bf16[768]{0:T(1024)(128)(2,1)} %param.20) | copy-start | bytes 4612
  37.5 22.4 %copy-start.3 = (bf16[768,192]{0,1:T(8,128)(2,1)S(1)}, bf16[768,192]{0,1:T(8,128)(2,1)}, u32[]{:S(2)}) copy-start(bf16[768,192]{0,1:T(8,128)(2,1)} %param.16) | copy-start | bytes 884740
  37.5 22.4 %all-to-all-start.1 = ((bf16[4,2,64,768]{3,2,1,0:T(8,128)(2,1)}), bf16[4,2,64,768]{3,2,1,0:T(8,128)(2,1)S(1)}, u32[]{:S(2)}, u32[]{:S(2)}) async-start(bf16[4,2,64,768]{3,2,1,0:T(8,128)(2,1)} %stack.3), calls=%async_computation.1 | async-start | bytes 1572864 | tf_op jit(solution)/shard_map/all_to_all | solution.py:52
  42.5 85.9 %all-reduce.4.cloned.1.call-start = ((), (), s32[]{:S(2)}) async-start(), calls=%async_computation.2 | async-start | bytes 1572864 | tf_op jit(solution)/shard_map/psum | solution.py:77
  78.9 1.2 copy-start.8
  81.5 1.0 copy-start.2
  82.4 1.7 copy-start.6
  83.8 97.3 %all-reduce.6.cloned.1.call-start = ((), (), s32[]{:S(2)}) async-start(), calls=%async_computation.3 | async-start | bytes 1572864
  128.5 1.5 copy-start.1
  130.4 1.3 copy-start.7
  136.1 1.8 copy-start.9
Sparse Core Ops, SparseCore 0:
  84.0 44.4 all-reduce.3
  138.0 43.1 all-reduce.5
